TPU v7x, 128 devices: a whole 4x4x4 slice. The times are simulated.
128 devices in a mesh: row: 16 (over z_lo, x, core), col: 4 (over y), head: 2 (over z_hi).
Axes of the slice: x: 4, y: 4, z: 4 (z_hi: 2, z_lo: 2; z = z_hi * 2 + z_lo), core: 2. Of those that a mesh axis runs over, the one named last changes fastest.
Arguments:
- query_map: bfloat16 [256, 128, 3072], P('row', 'col', 'head'), may hold values from -6 to 6
- key_map: bfloat16 [256, 128, 3072], P('row', 'col', 'head'), may hold values from -7 to 7
- value_map: bfloat16 [256, 128, 3072], P('row', 'col', 'head'), may hold values from -6 to 6
- window_mask: int32 [16, 4, 13, 13], P('row', 'col'), may hold values 0 or 1
- tile_radius: int32 [16, 4], P('row', 'col'), may hold values from 3 to 6, as said below
- dilation_per_tile: int32 [16, 4], P('row', 'col'), may hold values from 1 to 3, as said below
- rel_bias: float32 [48, 13, 13], P('head'), may hold values from -4 to 4
- out_weight: bfloat16 [3072, 3072], P('head'), may hold values from -0.109375 to 0.109375
Outputs:
- mixed: bfloat16 [256, 128, 3072], P('row', 'col', 'head')
Inputs may be any that keep to these rules, and one draw needn't show every extreme that they name: `tile_radius`: in each row of tiles, at least one tile has radius 6 and dilation 3. `dilation_per_tile`: in each row of tiles, at least one tile has radius 6 and dilation 3.
All inputs are finite; a program needn't handle non-finite values. No bound on the sum of `window_mask` on one device may be relied on, other than what follows from the above.
Results may differ from a plain program's by a relative error of at most 0.0073.
Values may be sent and summed in bfloat16 or wider, within the bound.
A program may use at most 384 MiB of HBM per device.

v0:
```python
import functools

import jax
import jax.numpy as jnp
from jax import lax
from jax.experimental import pallas as pl
from jax.experimental.pallas import tpu as pltpu
from jax.sharding import PartitionSpec as P

HEAD_DIM = 64
RADIUS_MAX = 6
WINDOW = 13
HALO = 18
NEG = -1e30
BLOCK_ROWS = 3
BLOCK_KEYS = 16
SIDE_COLS = 24
GROUP = 4
LANES = GROUP * HEAD_DIM
BLOCKS = 6
SLOTS = BLOCKS * BLOCK_ROWS


MESH = pl.DeviceIdType.MESH


def shifted(value, axis, steps):
    count = lax.axis_size(axis)
    leading, last = (max(0, -steps), min(count, count - steps))
    return lax.ppermute(value, axis, [(source, source + steps) for source in range(leading, last)])


def spread_bias(pattern, radius, rel_bias, first, last):
    heads = rel_bias.shape[0]
    steps = jnp.abs(jnp.arange(WINDOW, dtype=jnp.int32) - RADIUS_MAX)
    centre = (steps[:, None] == 0) & (steps[None, :] == 0)
    near = (steps[:, None] <= radius) & (steps[None, :] <= radius)
    used = ((pattern == 1) | centre) & near
    masked = jnp.where(used[None], rel_bias, NEG)
    turned = jnp.swapaxes(masked, 1, 2)[:, first:last]
    extra = BLOCK_KEYS - WINDOW
    turned = jnp.pad(turned, ((0, 0), (0, 0), (BLOCK_ROWS - 1, extra)), constant_values=NEG)
    parts = [turned[:, :, BLOCK_ROWS - 1 - t :][:, :, :BLOCK_KEYS] for t in range(BLOCK_ROWS)]
    count = BLOCK_ROWS * (last - first)
    flat = jnp.stack(parts, axis=1).reshape(heads * count, BLOCK_KEYS)
    width = BLOCK_KEYS * 32
    lane_row = jnp.arange(width, dtype=jnp.int32)[None, :] // 32
    spread = (lane_row == jnp.arange(BLOCK_KEYS, dtype=jnp.int32)[:, None]).astype(jnp.float32)
    wide = jnp.dot(flat, spread, precision=lax.Precision.HIGHEST)
    return wide.reshape(heads, count, width)


def fill_table(cols, offset, first, last, d, x_ref, t_ref):
    width = x_ref.shape[2]
    lane = lax.broadcasted_iota(jnp.int32, (cols, width), 1)
    rel = lane % 32 - lax.broadcasted_iota(jnp.int32, (cols, width), 0) + offset
    count = last - first

    @pl.loop(0, x_ref.shape[0])
    def _(h):
        rows = x_ref[h]
        for t in range(BLOCK_ROWS):
            acc = jnp.full((cols, width), NEG, jnp.float32)
            for b in range(count):
                row = rows[t * count + b : t * count + b + 1]
                acc = jnp.where(rel == (b + first - RADIUS_MAX) * d, row, acc)
            t_ref[h, t] = acc


def base_row(beta, d):
    two = beta % 2 + 6 * (beta // 2)
    three = beta % 3 + 9 * (beta // 3)
    return jnp.where(d == 1, 3 * beta, jnp.where(d == 2, two, three))


def one_set(d, row_anchor, total_rows, group, beta, load_q, t_ref, store_o, l_ref, k_ref, v_ref, s_ref, p_ref):
    cols = t_ref.shape[2]
    base = base_row(beta, d)
    span = k_ref.shape[0]
    depth = span - 2 * HALO
    width = BLOCK_KEYS * 32
    queries = []
    for t in range(BLOCK_ROWS):
        row = jnp.minimum(base + t * d, depth - 1)
        queries.append(load_q(row).astype(jnp.float32) * 0.125)
    queries = jnp.concatenate(queries, axis=0)
    lane_head = lax.broadcasted_iota(jnp.int32, queries.shape, 1) // HEAD_DIM
    spread = [jnp.where(lane_head == h, queries, 0.0) for h in range(GROUP)]
    spread = jnp.concatenate(spread, axis=0).astype(jnp.bfloat16)
    key_rows = []
    value_rows = []
    for u in range(BLOCK_KEYS):
        row = jnp.clip(HALO + base + (u - RADIUS_MAX) * d, 0, span - 1)
        key_rows.append(k_ref[row])
        value_rows.append(v_ref[row])
    keys = jnp.concatenate(key_rows, axis=0)
    values = jnp.concatenate(value_rows, axis=0)
    s_ref[...] = lax.dot_general(
        spread, keys, (((1,), (1,)), ((), ())), preferred_element_type=jnp.float32
    )
    step = lax.broadcasted_iota(jnp.int32, (1, width), 1) // 32
    key_row = row_anchor + base + (step - RADIUS_MAX) * d
    row_bias = jnp.where((key_row >= 0) & (key_row < total_rows), 0.0, NEG)
    sums = []
    peaks = []
    for h in range(GROUP):
        for t in range(BLOCK_ROWS):
            at = (h * BLOCK_ROWS + t) * cols
            score = s_ref[at : at + cols] + (t_ref[group * GROUP + h, t] + row_bias)
            peak = jnp.maximum(jnp.max(score, axis=1, keepdims=True), -1e20)
            weight = jnp.exp(score - peak)
            sums.append(jnp.sum(weight, axis=1, keepdims=True))
            peaks.append(peak)
            p_ref[at : at + cols] = weight.astype(jnp.bfloat16)
    mixed = jnp.dot(p_ref[...], values, preferred_element_type=jnp.float32)
    head_of = lax.broadcasted_iota(jnp.int32, (cols, LANES), 1) // HEAD_DIM
    stat_lane = lax.broadcasted_iota(jnp.int32, (cols, 128), 1)
    for t in range(BLOCK_ROWS):
        slot = beta * BLOCK_ROWS + t
        out = jnp.zeros((cols, LANES), jnp.float32)
        stats = l_ref[slot]
        for h in range(GROUP):
            at = h * BLOCK_ROWS + t
            total = sums[at]
            some = total > 0.0
            inverse = 1.0 / jnp.where(some, total, 1.0)
            out = jnp.where(head_of == h, mixed[at * cols : (at + 1) * cols] * inverse, out)
            lse = jnp.where(some, peaks[at] + jnp.log(jnp.where(some, total, 1.0)), NEG)
            stats = jnp.where(stat_lane == group * GROUP + h, lse, stats)
        store_o(slot, out.astype(jnp.bfloat16))
        l_ref[slot] = stats


def window_kernel(
    total_rows, groups, tiny, q_ref, k_own, v_own, x_o, x_l, x_r,
    o_own, l_own, back_l, back_r, lse_l, lse_r,
    win_k, win_v, k_ref, v_ref, land_l, land_r, q_l, q_r, t_o, t_l, t_r,
    s_o, s_l, s_r, p_o, p_l, p_r, out_l, out_r, st_l, st_r,
    send, recv, back_send, back_recv,
):
    row, col = lax.axis_index("row"), lax.axis_index("col")
    rows, cols_n = lax.axis_size("row"), lax.axis_size("col")
    depth, cols, _ = k_own.shape
    spill = HALO - depth
    side = land_l.shape[2]

    for edge, at, n in (
        (row < 2, 0, spill),
        (row < 1, spill, depth),
        (row > rows - 2, HALO, depth),
        (row > rows - 3, HALO + depth, spill),
    ):
        @pl.when(edge)
        def _():
            for ref in (win_k, win_v):
                ref[:, at : at + n] = jnp.zeros((groups, n, cols, LANES), ref.dtype)
    for edge, ref in ((col < 1, land_l), (col > cols_n - 2, land_r)):
        @pl.when(edge)
        def _():
            ref[...] = jnp.zeros_like(ref)

    peers = (
        (row < rows - 1, {"row": row + 1}),
        (row > 0, {"row": row - 1}),
        (row < rows - 2, {"row": row + 2}),
        (row > 1, {"row": row - 2}),
        (col < cols_n - 1, {"col": col + 1}),
        (col > 0, {"col": col - 1}),
    )
    barrier = pltpu.get_barrier_semaphore()
    count = 0
    for there, peer in peers:
        count = count + there.astype(jnp.int32)

        @pl.when(there)
        def _():
            pl.semaphore_signal(barrier, inc=1, device_id=peer, device_id_type=MESH)
    pl.semaphore_wait(barrier, count)

    def copies(g):
        at = pl.ds(pl.multiple_of(g * LANES, LANES), LANES)
        plan = []
        for own, win in ((k_own, win_k), (v_own, win_v)):
            plan += [
                (0, 1, own.at[:, :, at], win.at[g, spill:HALO]),
                (1, 0, own.at[:, :, at], win.at[g, HALO : HALO + depth]),
                (2, 3, own.at[depth - spill : depth, :, at], win.at[g, 0:spill]),
                (3, 2, own.at[0:spill, :, at], win.at[g, HALO + depth : 2 * HALO]),
            ]
        plan += [
            (4, 5, q_ref.at[:, cols - side : cols, at], land_l.at[g]),
            (5, 4, q_ref.at[:, 0:side, at], land_r.at[g]),
        ]
        made = []
        for n, (to, frm, src, dst) in enumerate(plan):
            there, peer = peers[to]
            made.append((there, peers[frm][0], pltpu.make_async_remote_copy(
                src_ref=src, dst_ref=dst, send_sem=send.at[g, n], recv_sem=recv.at[g, n],
                device_id=peer, device_id_type=MESH,
            )))
        return made

    def backs(g):
        made = []
        for n, (to, frm, src, dst) in enumerate(((5, 4, out_l, back_r), (4, 5, out_r, back_l))):
            there, peer = peers[to]
            made.append((there, peers[frm][0], pltpu.make_async_remote_copy(
                src_ref=src.at[g], dst_ref=dst.at[g], send_sem=back_send.at[g, n],
                recv_sem=back_recv.at[g, n], device_id=peer, device_id_type=MESH,
            )))
        return made

    def lses():
        made = []
        for n, (to, frm, src, dst) in enumerate(((5, 4, st_l, lse_r), (4, 5, st_r, lse_l))):
            there, peer = peers[to]
            made.append((there, peers[frm][0], pltpu.make_async_remote_copy(
                src_ref=src, dst_ref=dst, send_sem=back_send.at[groups, n],
                recv_sem=back_recv.at[groups, n], device_id=peer, device_id_type=MESH,
            )))
        return made

    def each(made, which, act):
        for entry in made:
            @pl.when(entry[which])
            def _():
                act(entry[2])

    @pl.loop(0, groups)
    def _(g):
        each(copies(g), 0, lambda copy: copy.start())

    fill_table(cols, 0, 0, WINDOW, tiny[0], x_o, t_o)
    fill_table(side, side, RADIUS_MAX + 1, WINDOW, tiny[1], x_l, t_l)
    fill_table(side, -cols, 0, RADIUS_MAX, tiny[2], x_r, t_r)
    for ref in (l_own, st_l, st_r):
        ref[...] = jnp.zeros_like(ref)
    anchor = row * depth

    @pl.loop(0, groups)
    def _(g):
        at = pl.ds(pl.multiple_of(g * LANES, LANES), LANES)
        each(copies(g), 1, lambda copy: copy.wait_recv())
        for ref, win, own in ((k_ref, win_k, k_own), (v_ref, win_v, v_own)):
            ref[0:HALO] = win[g, 0:HALO]
            ref[HALO : HALO + depth] = own[:, :, at]
            ref[HALO + depth : 2 * HALO + depth] = win[g, HALO : 2 * HALO]
        q_l[...] = land_l[g]
        q_r[...] = land_r[g]

        @pl.when(g > 0)
        def _():
            each(backs(g - 1), 0, lambda copy: copy.start())

        def put_own(slot, value):
            o_own[slot, :, at] = value

        def put_left(slot, value):
            out_l[g, slot] = value

        def put_right(slot, value):
            out_r[g, slot] = value

        @pl.loop(0, BLOCKS)
        def _(beta):
            one_set(tiny[0], anchor, total_rows, g, beta, lambda i: q_ref[i, :, at], t_o, put_own, l_own, k_ref, v_ref, s_o, p_o)
            one_set(tiny[1], anchor, total_rows, g, beta, lambda i: q_l[i], t_l, put_left, st_l, k_ref, v_ref, s_l, p_l)
            one_set(tiny[2], anchor, total_rows, g, beta, lambda i: q_r[i], t_r, put_right, st_r, k_ref, v_ref, s_r, p_r)

    each(backs(groups - 1), 0, lambda copy: copy.start())
    each(lses(), 0, lambda copy: copy.start())

    @pl.loop(0, groups)
    def _(g):
        each(copies(g), 0, lambda copy: copy.wait_send())
        each(backs(g), 0, lambda copy: copy.wait_send())
        each(backs(g), 1, lambda copy: copy.wait_recv())
    each(lses(), 0, lambda copy: copy.wait_send())
    each(lses(), 1, lambda copy: copy.wait_recv())


def window_attention(tiny, total_rows, q, k, v, wide):
    depth, cols, features = q.shape
    groups = features // LANES
    heads = groups * GROUP
    keys = BLOCK_KEYS * 32
    counts = (cols, SIDE_COLS, SIDE_COLS)
    vmem = pl.BlockSpec(memory_space=pltpu.VMEM)
    hbm = pl.BlockSpec(memory_space=pl.ANY)
    bf16, f32 = jnp.bfloat16, jnp.float32
    dma = pltpu.SemaphoreType.DMA
    return pl.pallas_call(
        functools.partial(window_kernel, total_rows, groups),
        in_specs=[pl.BlockSpec(memory_space=pltpu.SMEM)] + [vmem] * 6,
        out_specs=[vmem, vmem, hbm, hbm, hbm, hbm],
        out_shape=[
            jax.ShapeDtypeStruct((SLOTS, cols, features), bf16),
            jax.ShapeDtypeStruct((SLOTS, cols, 128), f32),
            jax.ShapeDtypeStruct((groups, SLOTS, SIDE_COLS, LANES), bf16),
            jax.ShapeDtypeStruct((groups, SLOTS, SIDE_COLS, LANES), bf16),
            jax.ShapeDtypeStruct((SLOTS, SIDE_COLS, 128), f32),
            jax.ShapeDtypeStruct((SLOTS, SIDE_COLS, 128), f32),
        ],
        scratch_shapes=[pltpu.VMEM((groups, 2 * HALO, cols, LANES), bf16)] * 2
        + [pltpu.VMEM((depth + 2 * HALO, cols, LANES), bf16)] * 2
        + [pltpu.VMEM((groups, depth, SIDE_COLS, LANES), bf16)] * 2
        + [pltpu.VMEM((depth, SIDE_COLS, LANES), bf16)] * 2
        + [pltpu.VMEM((heads, BLOCK_ROWS, n, keys), f32) for n in counts]
        + [pltpu.VMEM((GROUP * BLOCK_ROWS * n, keys), f32) for n in counts]
        + [pltpu.VMEM((GROUP * BLOCK_ROWS * n, keys), bf16) for n in counts]
        + [pltpu.VMEM((groups, SLOTS, SIDE_COLS, LANES), bf16)] * 2
        + [pltpu.VMEM((SLOTS, SIDE_COLS, 128), f32)] * 2
        + [dma((groups, 10)), dma((groups, 10)), dma((groups + 1, 2)), dma((groups + 1, 2))],
        compiler_params=pltpu.CompilerParams(
            collective_id=0, has_side_effects=True, vmem_limit_bytes=62 * 2**20
        ),
        cost_estimate=pl.CostEstimate(flops=2 * 10**10, bytes_accessed=4 * 10**7, transcendentals=0),
        name="window_attention",
    )(tiny, q, k, v, *wide)


def merge_kernel(places, slots, flags, own, left, right, l_o, l_l, l_r, w_ref, a_ref, part_ref):
    step = pl.program_id(0)
    rows = 4
    cols = own.shape[1]
    features = own.shape[2]
    groups = left.shape[0]
    pick = lax.broadcasted_iota(jnp.int32, (128, features), 1) // HEAD_DIM
    pick = (pick == lax.broadcasted_iota(jnp.int32, (128, features), 0)).astype(jnp.bfloat16)
    tail = cols - l_l.shape[1]
    has_left, has_right = flags[0] > 0, flags[1] > 0

    def lay(value, ahead, fill):
        blank = jnp.full((tail, value.shape[1]), fill, jnp.float32)
        return jnp.concatenate([blank, value] if ahead else [value, blank], axis=0)

    def whole(ref, slot, there):
        value = jnp.concatenate([ref[g, slot].astype(jnp.float32) for g in range(groups)], axis=1)
        return jnp.where(there, value, 0.0)

    first, second, third = [], [], []
    mine, lefts, rights = [], [], []
    for i in range(rows):
        slot = slots[step * rows + i]
        a = l_o[slot]
        b = jnp.where(has_left, lay(l_l[slot], False, NEG), NEG)
        c = jnp.where(has_right, lay(l_r[slot], True, NEG), NEG)
        top = jnp.maximum(jnp.maximum(a, b), c)
        a, b, c = jnp.exp(a - top), jnp.exp(b - top), jnp.exp(c - top)
        total = a + b + c
        first.append(a / total)
        second.append(b / total)
        third.append(c / total)
        mine.append(own[slot].astype(jnp.float32))
        lefts.append(lay(whole(left, slot, has_left), False, 0.0))
        rights.append(lay(whole(right, slot, has_right), True, 0.0))

    def wide(parts):
        value = jnp.concatenate(parts, axis=0)
        high = value.astype(jnp.bfloat16)
        low = (value - high.astype(jnp.float32)).astype(jnp.bfloat16)
        dot = lambda x: jnp.dot(x, pick, preferred_element_type=jnp.float32)
        return dot(high) + dot(low)

    total = wide(first) * jnp.concatenate(mine, axis=0)
    total = total + wide(second) * jnp.concatenate(lefts, axis=0)
    total = total + wide(third) * jnp.concatenate(rights, axis=0)
    attended = total.astype(jnp.bfloat16)
    a_ref[...] = attended
    part_ref[...] = jnp.dot(attended, w_ref[...], preferred_element_type=jnp.float32).astype(jnp.bfloat16)


def merge(peer, slots, flags, arrays, weight, depth):
    own = arrays[0]
    cols, features = own.shape[1:]
    rows = 4
    half = weight.shape[1] // 2
    full = lambda arr: pl.BlockSpec(arr.shape, lambda i, *_: (0,) * arr.ndim)
    flat = lambda n: pl.BlockSpec((rows * cols, n), lambda i, *_: (i, 0))
    return pl.pallas_call(
        merge_kernel,
        grid_spec=pltpu.PrefetchScalarGridSpec(
            num_scalar_prefetch=3,
            grid=(depth // rows,),
            in_specs=[full(arr) for arr in arrays]
            + [pl.BlockSpec((features, half), lambda i, p, *_: (0, p[0]))],
            out_specs=[flat(features), flat(half)],
        ),
        out_shape=[
            jax.ShapeDtypeStruct((depth * cols, features), jnp.bfloat16),
            jax.ShapeDtypeStruct((depth * cols, half), jnp.bfloat16),
        ],
        compiler_params=pltpu.CompilerParams(vmem_limit_bytes=56 * 2**20),
        cost_estimate=pl.CostEstimate(flops=3 * 10**9, bytes_accessed=2 * 10**7, transcendentals=0),
        name="merge_project",
    )(peer, slots, flags, *arrays, weight)


def shards(query_map, key_map, value_map, window_mask, tile_radius, dilation_per_tile, rel_bias, out_weight):
    depth, cols, features = query_map.shape
    total_rows = depth * lax.axis_size("row")
    settings = jnp.concatenate(
        [window_mask.reshape(-1), tile_radius.reshape(-1), dilation_per_tile.reshape(-1)]
    )
    from_left = shifted(settings, "col", 1)
    from_right = shifted(settings, "col", -1)
    wide = []
    dilations = []
    for values, first, last in (
        (settings, 0, WINDOW),
        (from_left, RADIUS_MAX + 1, WINDOW),
        (from_right, 0, RADIUS_MAX),
    ):
        pattern = values[:-2].reshape(WINDOW, WINDOW)
        dilations.append(jnp.maximum(values[-1], 1))
        wide.append(spread_bias(pattern, values[-2], rel_bias, first, last))
    tiny = jnp.stack(dilations).astype(jnp.int32)
    arrays = window_attention(tiny, total_rows, query_map, key_map, value_map, wide)
    o_own, l_own, back_l, back_r, lse_l, lse_r = arrays
    d = dilations[0]
    index = jnp.arange(depth, dtype=jnp.int32)
    turn = index // d
    slots = (d * (turn // BLOCK_ROWS) + index % d) * BLOCK_ROWS + turn % BLOCK_ROWS
    col = lax.axis_index("col")
    head = lax.axis_index("head")
    flags = jnp.stack([col > 0, col < lax.axis_size("col") - 1]).astype(jnp.int32)
    attended, theirs = merge(
        (1 - head).astype(jnp.int32).reshape(1), slots.astype(jnp.int32), flags,
        (o_own, back_l, back_r, l_own, lse_l, lse_r), out_weight, depth,
    )
    arrived = lax.ppermute(theirs, "head", [(0, 1), (1, 0)])
    half = out_weight.shape[1] // 2
    my_weight = lax.dynamic_slice_in_dim(out_weight, head * half, half, 1)
    mine = jnp.dot(attended, my_weight, preferred_element_type=jnp.float32)
    mine, arrived = lax.optimization_barrier((mine, arrived))
    return (mine + arrived.astype(jnp.float32)).astype(jnp.bfloat16).reshape(depth, cols, half)


def solution(mesh):
    placed = (
        P("row", "col", "head"),
        P("row", "col", "head"),
        P("row", "col", "head"),
        P("row", "col", None, None),
        P("row", "col"),
        P("row", "col"),
        P("head", None, None),
        P("head", None),
    )
    return jax.shard_map(
        shards, mesh=mesh, in_specs=placed, out_specs=P("row", "col", "head"), check_vma=False
    )
```

profile of v0, /device:TPU:40, one launch (start us, length us, event | category | flops | bytes accessed | tf_op | source)
XLA Modules:
  0.0 149.4 jit_solution(9635481486655944452)
XLA Ops:
  1.3 0.7 reduce
  2.0 0.1 reshape.301
  2.1 0.1 pad_add_fusion
  2.2 2.4 %collective-permute-start.1 = (s32[171]{0:T(256)S(1)}, s32[171]{0:T(256)S(1)}, u32[]{:S(2)}, u32[]{:S(2)}) collective-permute-start(s32[171]{0:T(256)S(1)} %pad_add_fusion), channel_id=1, source_target_pairs={{2,0},{4,2},{6,4},{3,1},{5,3},{7,5},{10,8},{12,10},{14,12},{11,9},... | collective-permute-start | bytes 2060 | tf_op jit(solution)/shard_map/ppermute | solution.py:30
  4.5 3.5 %collective-permute-start = (s32[171]{0:T(256)S(1)}, s32[171]{0:T(256)S(1)}, u32[]{:S(2)}, u32[]{:S(2)}) collective-permute-start(s32[171]{0:T(256)S(1)} %pad_add_fusion), channel_id=1, source_target_pairs={{0,2},{2,4},{4,6},{1,3},{3,5},{5,7},{8,10},{10,12},{12,14},{9,11},... | collective-permute-start | bytes 2060 | tf_op jit(solution)/shard_map/ppermute | solution.py:30
  8.0 0.7 broadcast_compare_fusion
  8.8 0.7 fusion.28.slots
  9.5 0.6 add_convert_fusion.1.flags
  10.1 0.0 collective-permute-done.1
  10.1 0.6 fusion.30
  10.7 0.7 broadcast_compare_fusion.1
  11.4 0.0 collective-permute-done
  11.4 0.7 fusion.31
  12.0 0.7 broadcast_compare_fusion.2
  12.7 0.1 eq.105
  12.8 0.1 eq.107
  12.9 0.1 fusion.23
  13.0 1.0 select_bitcast_fusion
  14.1 0.1 copy.14
  14.3 0.2 copy.15
  14.6 0.2 copy.22
  14.8 2.3 %fusion.16.x_o = f32[24,39,512]{2,1,0:T(8,128)} fusion(f32[24,39,16]{1,2,0:T(8,128)S(1)} %copy.15, s32[512]{0:T(512)S(1)} %add_select_fusion), kind=kOutput, calls=%fused_computation.31 | convolution fusion | flops 92020736 | bytes 1978880 | tf_op jit(solution)/shard_map/dot_general | solution.py:49
  17.1 1.7 %fusion.12.x_r = f32[24,18,512]{2,1,0:T(8,128)} fusion(f32[24,18,16]{1,2,0:T(8,128)S(1)} %copy.22, s32[512]{0:T(512)S(1)} %add_select_fusion), kind=kOutput, calls=%fused_computation.29 | convolution fusion | flops 42475520 | bytes 914432 | tf_op jit(solution)/shard_map/dot_general | solution.py:49
  18.9 0.2 copy.20
  19.1 1.7 %fusion.14.x_l = f32[24,18,512]{2,1,0:T(8,128)} fusion(f32[24,18,16]{1,2,0:T(8,128)S(1)} %copy.20, s32[512]{0:T(512)S(1)} %add_select_fusion), kind=kOutput, calls=%fused_computation.30 | convolution fusion | flops 42475520 | bytes 914432 | tf_op jit(solution)/shard_map/dot_general | solution.py:49
  22.1 0.7 pad_add_fusion.1.tiny
  22.8 75.8 %window_attention.1 = (bf16[18,32,1536]{2,1,0:T(8,128)(2,1)}, f32[18,32,128]{2,1,0:T(8,128)}, bf16[6,18,24,256]{3,2,1,0:T(8,128)(2,1)}, bf16[6,18,24,256]{3,2,1,...) custom-call(s32[3]{0:T(128)} %pad_add_fusion.1.tiny, bf16[16,32,1536]{2,1,0:T(8,128)(2,1)} %q_ref.1, ...), custom_call_target="tpu_custom_call" | custom-call | flops 20000000000 | bytes 40000000 | tf_op jit(solution)/shard_map/window_attention/pallas_call | solution.py:292
  98.5 11.5 %merge_project.1 = (bf16[512,1536]{1,0:T(8,128)(2,1)}, bf16[512,1536]{1,0:T(8,128)(2,1)}) custom-call(s32[1]{0:T(128)} %bitcast.places, s32[16]{0:T(128)} %fusion.28.slots, s32[2]{0:T(128)} %add_convert_fusion.1.flags, bf16[18,32,1536]{2,1,0:T(8,128)(2,1)} %get-tuple-element.15.own, bf16[6,18,24,256]{3,2,1,0:T(8,128)(2,1)} %get-tuple-element.16.left, ...), custom_call_target="tpu_custom_call" | custom-call | flops 3000000000 | bytes 20000000 | tf_op jit(solution)/shard_map/merge_project/pallas_call | solution.py:380
  110.0 3.0 %collective-permute-start.2 = (bf16[512,1536]{1,0:T(8,128)(2,1)}, bf16[512,1536]{1,0:T(8,128)(2,1)S(1)}, u32[]{:S(2)}, u32[]{:S(2)}) collective-permute-start(bf16[512,1536]{1,0:T(8,128)(2,1)} %get-tuple-element.22), channel_id=1, source_target_pairs={{0,1},{1,0},{2,3},{3,2},{4,5},{5,4},{6,7},{7,6},{8,9},{9,8},{10,11... | collective-permute-start | bytes 4718600 | tf_op jit(solution)/shard_map/ppermute | solution.py:431
  113.0 4.9 %fusion = f32[512,1536]{1,0:T(8,128)S(1)} fusion(bf16[512,1536]{1,0:T(8,128)(2,1)} %get-tuple-element.21, bf16[1536,3072]{1,0:T(8,128)(2,1)} %w_ref.1, s32[]{:T(128)S(6)} %select_n.62), kind=kOutput, calls=%fused_computation | convolution fusion | flops 2415919104 | bytes 9437188 | tf_op jit(solution)/shard_map/dot_general | solution.py:434
  118.0 29.7 %collective-permute-done.2 = bf16[512,1536]{1,0:T(8,128)(2,1)S(1)} collective-permute-done((bf16[512,1536]{1,0:T(8,128)(2,1)}, bf16[512,1536]{1,0:T(8,128)(2,1)S(1)}, u32[]{:S(2)}, u32[]{:S(2)}) %collective-permute-start.2) | collective-permute-done | bytes 1572896 | tf_op jit(solution)/shard_map/ppermute | solution.py:431
  147.6 1.7 %add_convert_fusion = bf16[512,1536]{1,0:T(8,128)(2,1)} fusion(f32[512,1536]{1,0:T(8,128)S(1)} %fusion, bf16[512,1536]{1,0:T(8,128)(2,1)S(1)} %collective-permute-done.2), kind=kLoop, calls=%fused_computation.2 | loop fusion | flops 2359296 | bytes 6291456 | tf_op jit(solution)/shard_map/convert_element_type | solution.py:436
  (14 shorter events, 0.2 us)
Async XLA Ops:
  2.2 7.9 %collective-permute-start.1 = (s32[171]{0:T(256)S(1)}, s32[171]{0:T(256)S(1)}, u32[]{:S(2)}, u32[]{:S(2)}) collective-permute-start(s32[171]{0:T(256)S(1)} %pad_add_fusion), channel_id=1, source_target_pairs={{2,0},{4,2},{6,4},{3,1},{5,3},{7,5},{10,8},{12,10},{14,12},{11,9},... | collective-permute-start | bytes 2060 | tf_op jit(solution)/shard_map/ppermute | solution.py:30
  4.5 6.8 %collective-permute-start = (s32[171]{0:T(256)S(1)}, s32[171]{0:T(256)S(1)}, u32[]{:S(2)}, u32[]{:S(2)}) collective-permute-start(s32[171]{0:T(256)S(1)} %pad_add_fusion), channel_id=1, source_target_pairs={{0,2},{2,4},{4,6},{1,3},{3,5},{5,7},{8,10},{10,12},{12,14},{9,11},... | collective-permute-start | bytes 2060 | tf_op jit(solution)/shard_map/ppermute | solution.py:30
  110.0 37.6 %collective-permute-start.2 = (bf16[512,1536]{1,0:T(8,128)(2,1)}, bf16[512,1536]{1,0:T(8,128)(2,1)S(1)}, u32[]{:S(2)}, u32[]{:S(2)}) collective-permute-start(bf16[512,1536]{1,0:T(8,128)(2,1)} %get-tuple-element.22), channel_id=1, source_target_pairs={{0,1},{1,0},{2,3},{3,2},{4,5},{5,4},{6,7},{7,6},{8,9},{9,8},{10,11... | collective-permute-start | bytes 4718600 | tf_op jit(solution)/shard_map/ppermute | solution.py:431
where the time goes:
time: 150 us; the launch traced here: 149 us
  Pallas kernels  87.3 us (58%)
  waiting for transfers between devices  29.7 us (20%)
  matrix products  10.7 us (7%)
  starting transfers between devices  8.82 us (6%)
  other arithmetic  7.75 us (5%)
  between operations  2.8 us (2%)
  local copies, waits for them, and re-layouts  2.35 us (2%)
    pallas_call x1, Pallas kernels, window_attention(): pl.pallas_call(functools.partial(window_kernel, total_rows, groups), in_s...  75.8 us
    ppermute x1, waiting for transfers between devices, shards(): arrived = lax.ppermute(theirs, 'head', [(0, 1), (1, 0)])  29.7 us
    pallas_call x1, Pallas kernels, merge(): pl.pallas_call(merge_kernel, grid_spec=pltpu.PrefetchScalarGridSpec(num_s...  11.5 us
    ppermute x2, starting transfers between devices, shifted(): lax.ppermute(value, axis, [(source, source + steps) for source in range(l...  5.84 us
    dot_general x3, matrix products, spread_bias(): wide = jnp.dot(flat, spread, precision=lax.Precision.HIGHEST)  5.74 us
    dot_general x1, matrix products, shards(): mine = jnp.dot(attended, my_weight, preferred_element_type=jnp.float32)  4.93 us
  transfers between devices with their start and end apart: 3, of which 1 were waited for; matrix products, arithmetic and copies ran while one was open for 6% of the time, Pallas kernels for 0%

commit v1 on v0

--- a/solution.py
+++ b/solution.py
@@ -42,29 +42,43 @@
     turned = jnp.pad(turned, ((0, 0), (0, 0), (BLOCK_ROWS - 1, extra)), constant_values=NEG)
     parts = [turned[:, :, BLOCK_ROWS - 1 - t :][:, :, :BLOCK_KEYS] for t in range(BLOCK_ROWS)]
     count = BLOCK_ROWS * (last - first)
-    flat = jnp.stack(parts, axis=1).reshape(heads * count, BLOCK_KEYS)
-    width = BLOCK_KEYS * 32
-    lane_row = jnp.arange(width, dtype=jnp.int32)[None, :] // 32
-    spread = (lane_row == jnp.arange(BLOCK_KEYS, dtype=jnp.int32)[:, None]).astype(jnp.float32)
-    wide = jnp.dot(flat, spread, precision=lax.Precision.HIGHEST)
-    return wide.reshape(heads, count, width)
-
-
-def fill_table(cols, offset, first, last, d, x_ref, t_ref):
-    width = x_ref.shape[2]
-    lane = lax.broadcasted_iota(jnp.int32, (cols, width), 1)
-    rel = lane % 32 - lax.broadcasted_iota(jnp.int32, (cols, width), 0) + offset
+    flat = jnp.stack(parts, axis=1).reshape(heads, count, BLOCK_KEYS)
+    flat = jnp.pad(flat, ((0, 0), (0, -count % 8), (0, 0)), constant_values=NEG)
+    return flat.reshape(-1, BLOCK_KEYS)
+
+
+def expand_bias(flat_ref, x_ref):
+    value = flat_ref[...]
+    high = value.astype(jnp.bfloat16)
+    rest = value - high.astype(jnp.float32)
+    middle = rest.astype(jnp.bfloat16)
+    low = (rest - middle.astype(jnp.float32)).astype(jnp.bfloat16)
+    width = x_ref.shape[1]
+    pick = lax.broadcasted_iota(jnp.int32, (BLOCK_KEYS, width), 1) // 32
+    pick = (pick == lax.broadcasted_iota(jnp.int32, (BLOCK_KEYS, width), 0)).astype(jnp.bfloat16)
+    dot = lambda part: jnp.dot(part, pick, preferred_element_type=jnp.float32)
+    x_ref[...] = dot(high) + dot(middle) + dot(low)
+
+
+def fill_table(offset, first, last, d, x_ref, t_ref):
+    heads, _, cols, width = t_ref.shape
+    stride = x_ref.shape[0] // heads
     count = last - first
 
-    @pl.loop(0, x_ref.shape[0])
+    @pl.loop(0, heads)
     def _(h):
-        rows = x_ref[h]
-        for t in range(BLOCK_ROWS):
-            acc = jnp.full((cols, width), NEG, jnp.float32)
-            for b in range(count):
-                row = rows[t * count + b : t * count + b + 1]
-                acc = jnp.where(rel == (b + first - RADIUS_MAX) * d, row, acc)
-            t_ref[h, t] = acc
+        rows = x_ref[pl.ds(pl.multiple_of(h * stride, 8), stride)]
+        for top in range(0, cols, 8):
+            lane = lax.broadcasted_iota(jnp.int32, (8, 128), 1)
+            rel = lane % 32 - lax.broadcasted_iota(jnp.int32, (8, 128), 0) + (offset - top)
+            masks = [rel == (b + first - RADIUS_MAX) * d for b in range(count)]
+            for t in range(BLOCK_ROWS):
+                for left in range(0, width, 128):
+                    acc = jnp.full((8, 128), NEG, jnp.float32)
+                    for b in range(count):
+                        at = t * count + b
+                        acc = jnp.where(masks[b], rows[at : at + 1, left : left + 128], acc)
+                    t_ref[h, t, top : top + 8, left : left + 128] = acc
 
 
 def base_row(beta, d):
@@ -131,18 +145,69 @@
         l_ref[slot] = stats
 
 
+def merge_rows(step, rows, slots, has_left, has_right, own, left, right, l_o, l_l, l_r):
+    cols, features = own.shape[1:]
+    groups = left.shape[0]
+    pick = lax.broadcasted_iota(jnp.int32, (128, features), 1) // HEAD_DIM
+    pick = (pick == lax.broadcasted_iota(jnp.int32, (128, features), 0)).astype(jnp.bfloat16)
+    tail = cols - l_l.shape[1]
+
+    def lay(value, ahead, fill):
+        blank = jnp.full((tail, value.shape[1]), fill, jnp.float32)
+        return jnp.concatenate([blank, value] if ahead else [value, blank], axis=0)
+
+    def whole(ref, slot, there):
+        value = jnp.concatenate([ref[g, slot].astype(jnp.float32) for g in range(groups)], axis=1)
+        return jnp.where(there, value, 0.0)
+
+    first, second, third = [], [], []
+    mine, lefts, rights = [], [], []
+    for i in range(rows):
+        slot = slots[step * rows + i]
+        a = l_o[slot]
+        b = jnp.where(has_left, lay(l_l[slot], False, NEG), NEG)
+        c = jnp.where(has_right, lay(l_r[slot], True, NEG), NEG)
+        top = jnp.maximum(jnp.maximum(a, b), c)
+        a, b, c = jnp.exp(a - top), jnp.exp(b - top), jnp.exp(c - top)
+        total = a + b + c
+        first.append(a / total)
+        second.append(b / total)
+        third.append(c / total)
+        mine.append(own[slot].astype(jnp.float32))
+        lefts.append(lay(whole(left, slot, has_left), False, 0.0))
+        rights.append(lay(whole(right, slot, has_right), True, 0.0))
+
+    def wide(parts):
+        value = jnp.concatenate(parts, axis=0)
+        high = value.astype(jnp.bfloat16)
+        low = (value - high.astype(jnp.float32)).astype(jnp.bfloat16)
+        dot = lambda x: jnp.dot(x, pick, preferred_element_type=jnp.float32)
+        return dot(high) + dot(low)
+
+    total = wide(first) * jnp.concatenate(mine, axis=0)
+    total = total + wide(second) * jnp.concatenate(lefts, axis=0)
+    total = total + wide(third) * jnp.concatenate(rights, axis=0)
+    return total.astype(jnp.bfloat16)
+
+
 def window_kernel(
-    total_rows, groups, tiny, q_ref, k_own, v_own, x_o, x_l, x_r,
-    o_own, l_own, back_l, back_r, lse_l, lse_r,
+    total_rows, groups, tiny, slots, q_ref, k_own, v_own, flat_o, flat_l, flat_r, w_hbm,
+    result,
+    o_own, l_own, back_l, back_r, lse_l, lse_r, w_theirs, w_mine, attended, parts, arrived, x_o, x_l, x_r,
     win_k, win_v, k_ref, v_ref, land_l, land_r, q_l, q_r, t_o, t_l, t_r,
     s_o, s_l, s_r, p_o, p_l, p_r, out_l, out_r, st_l, st_r,
-    send, recv, back_send, back_recv,
+    send, recv, back_send, back_recv, head_send, head_recv, w_sem,
 ):
-    row, col = lax.axis_index("row"), lax.axis_index("col")
+    row, col, head = lax.axis_index("row"), lax.axis_index("col"), lax.axis_index("head")
     rows, cols_n = lax.axis_size("row"), lax.axis_size("col")
     depth, cols, _ = k_own.shape
     spill = HALO - depth
     side = land_l.shape[2]
+    half = w_mine.shape[1]
+    weights = [
+        pltpu.make_async_copy(w_hbm.at[:, pl.ds(pl.multiple_of(which * half, 128), half)], dst, w_sem.at[n])
+        for n, (which, dst) in enumerate(((1 - head, w_theirs), (head, w_mine)))
+    ]
 
     for edge, at, n in (
         (row < 2, 0, spill),
@@ -168,7 +233,8 @@
         (col > 0, {"col": col - 1}),
     )
     barrier = pltpu.get_barrier_semaphore()
-    count = 0
+    pl.semaphore_signal(barrier, inc=1, device_id={"head": 1 - head}, device_id_type=MESH)
+    count = 1
     for there, peer in peers:
         count = count + there.astype(jnp.int32)
 
@@ -230,9 +296,13 @@
     def _(g):
         each(copies(g), 0, lambda copy: copy.start())
 
-    fill_table(cols, 0, 0, WINDOW, tiny[0], x_o, t_o)
-    fill_table(side, side, RADIUS_MAX + 1, WINDOW, tiny[1], x_l, t_l)
-    fill_table(side, -cols, 0, RADIUS_MAX, tiny[2], x_r, t_r)
+    for copy in weights:
+        copy.start()
+    for flat, wide in ((flat_o, x_o), (flat_l, x_l), (flat_r, x_r)):
+        expand_bias(flat, wide)
+    fill_table(0, 0, WINDOW, tiny[0], x_o, t_o)
+    fill_table(side, RADIUS_MAX + 1, WINDOW, tiny[1], x_l, t_l)
+    fill_table(-cols, 0, RADIUS_MAX, tiny[2], x_r, t_r)
     for ref in (l_own, st_l, st_r):
         ref[...] = jnp.zeros_like(ref)
     anchor = row * depth
@@ -267,41 +337,93 @@
             one_set(tiny[1], anchor, total_rows, g, beta, lambda i: q_l[i], t_l, put_left, st_l, k_ref, v_ref, s_l, p_l)
             one_set(tiny[2], anchor, total_rows, g, beta, lambda i: q_r[i], t_r, put_right, st_r, k_ref, v_ref, s_r, p_r)
 
-    each(backs(groups - 1), 0, lambda copy: copy.start())
-    each(lses(), 0, lambda copy: copy.start())
+    for copy in weights:
+        copy.wait()
 
     @pl.loop(0, groups)
     def _(g):
         each(copies(g), 0, lambda copy: copy.wait_send())
+
+    each(backs(groups - 1), 0, lambda copy: copy.start())
+    each(lses(), 0, lambda copy: copy.start())
+
+    @pl.loop(0, groups)
+    def _(g):
+        each(backs(g), 1, lambda copy: copy.wait_recv())
+
+    each(lses(), 1, lambda copy: copy.wait_recv())
+
+    def swap(i):
+        return pltpu.make_async_remote_copy(
+            src_ref=parts.at[i], dst_ref=arrived.at[i], send_sem=head_send.at[i], recv_sem=head_recv.at[i],
+            device_id={"head": 1 - head}, device_id_type=MESH,
+        )
+
+    steps = parts.shape[0]
+
+    @pl.loop(0, steps)
+    def _(i):
+        attended[i] = merge_rows(
+            i, depth // steps, slots, col > 0, col < cols_n - 1, o_own, back_l, back_r, l_own, lse_l, lse_r
+        )
+
+        @pl.when(i > 0)
+        def _():
+            swap(i - 1).start()
+
+        parts[i] = jnp.dot(attended[i], w_theirs[...], preferred_element_type=jnp.float32).astype(jnp.bfloat16)
+
+    @pl.loop(0, groups)
+    def _(g):
         each(backs(g), 0, lambda copy: copy.wait_send())
-        each(backs(g), 1, lambda copy: copy.wait_recv())
+
     each(lses(), 0, lambda copy: copy.wait_send())
-    each(lses(), 1, lambda copy: copy.wait_recv())
-
-
-def window_attention(tiny, total_rows, q, k, v, wide):
+    swap(steps - 1).start()
+
+    @pl.loop(0, steps)
+    def _(i):
+        mine = jnp.dot(attended[i], w_mine[...], preferred_element_type=jnp.float32)
+        swap(i).wait_recv()
+        result[i] = (mine + arrived[i].astype(jnp.float32)).astype(jnp.bfloat16)
+
+    @pl.loop(0, steps)
+    def _(i):
+        swap(i).wait_send()
+
+
+def window_attention(tiny, slots, total_rows, q, k, v, flats, weight):
     depth, cols, features = q.shape
     groups = features // LANES
     heads = groups * GROUP
     keys = BLOCK_KEYS * 32
+    half = weight.shape[1] // 2
+    steps = 4
+    tokens = depth * cols // steps
     counts = (cols, SIDE_COLS, SIDE_COLS)
     vmem = pl.BlockSpec(memory_space=pltpu.VMEM)
-    hbm = pl.BlockSpec(memory_space=pl.ANY)
+    smem = pl.BlockSpec(memory_space=pltpu.SMEM)
     bf16, f32 = jnp.bfloat16, jnp.float32
     dma = pltpu.SemaphoreType.DMA
     return pl.pallas_call(
         functools.partial(window_kernel, total_rows, groups),
-        in_specs=[pl.BlockSpec(memory_space=pltpu.SMEM)] + [vmem] * 6,
-        out_specs=[vmem, vmem, hbm, hbm, hbm, hbm],
-        out_shape=[
-            jax.ShapeDtypeStruct((SLOTS, cols, features), bf16),
-            jax.ShapeDtypeStruct((SLOTS, cols, 128), f32),
-            jax.ShapeDtypeStruct((groups, SLOTS, SIDE_COLS, LANES), bf16),
-            jax.ShapeDtypeStruct((groups, SLOTS, SIDE_COLS, LANES), bf16),
-            jax.ShapeDtypeStruct((SLOTS, SIDE_COLS, 128), f32),
-            jax.ShapeDtypeStruct((SLOTS, SIDE_COLS, 128), f32),
-        ],
-        scratch_shapes=[pltpu.VMEM((groups, 2 * HALO, cols, LANES), bf16)] * 2
+        in_specs=[smem, smem] + [vmem] * 6 + [pl.BlockSpec(memory_space=pl.ANY)],
+        out_specs=vmem,
+        out_shape=jax.ShapeDtypeStruct((steps, tokens, half), bf16),
+        scratch_shapes=[
+            pltpu.VMEM((SLOTS, cols, features), bf16),
+            pltpu.VMEM((SLOTS, cols, 128), f32),
+            pltpu.VMEM((groups, SLOTS, SIDE_COLS, LANES), bf16),
+            pltpu.VMEM((groups, SLOTS, SIDE_COLS, LANES), bf16),
+            pltpu.VMEM((SLOTS, SIDE_COLS, 128), f32),
+            pltpu.VMEM((SLOTS, SIDE_COLS, 128), f32),
+            pltpu.VMEM((features, half), bf16),
+            pltpu.VMEM((features, half), bf16),
+            pltpu.VMEM((steps, tokens, features), bf16),
+            pltpu.VMEM((steps, tokens, half), bf16),
+            pltpu.VMEM((steps, tokens, half), bf16),
+        ]
+        + [pltpu.VMEM((flat.shape[0], keys), f32) for flat in flats]
+        + [pltpu.VMEM((groups, 2 * HALO, cols, LANES), bf16)] * 2
         + [pltpu.VMEM((depth + 2 * HALO, cols, LANES), bf16)] * 2
         + [pltpu.VMEM((groups, depth, SIDE_COLS, LANES), bf16)] * 2
         + [pltpu.VMEM((depth, SIDE_COLS, LANES), bf16)] * 2
@@ -310,90 +432,14 @@
         + [pltpu.VMEM((GROUP * BLOCK_ROWS * n, keys), bf16) for n in counts]
         + [pltpu.VMEM((groups, SLOTS, SIDE_COLS, LANES), bf16)] * 2
         + [pltpu.VMEM((SLOTS, SIDE_COLS, 128), f32)] * 2
-        + [dma((groups, 10)), dma((groups, 10)), dma((groups + 1, 2)), dma((groups + 1, 2))],
+        + [dma((groups, 10)), dma((groups, 10)), dma((groups + 1, 2)), dma((groups + 1, 2))]
+        + [dma((steps,)), dma((steps,)), dma((2,))],
         compiler_params=pltpu.CompilerParams(
-            collective_id=0, has_side_effects=True, vmem_limit_bytes=62 * 2**20
+            collective_id=0, has_side_effects=True, vmem_limit_bytes=67_000_000
         ),
         cost_estimate=pl.CostEstimate(flops=2 * 10**10, bytes_accessed=4 * 10**7, transcendentals=0),
         name="window_attention",
-    )(tiny, q, k, v, *wide)
-
-
-def merge_kernel(places, slots, flags, own, left, right, l_o, l_l, l_r, w_ref, a_ref, part_ref):
-    step = pl.program_id(0)
-    rows = 4
-    cols = own.shape[1]
-    features = own.shape[2]
-    groups = left.shape[0]
-    pick = lax.broadcasted_iota(jnp.int32, (128, features), 1) // HEAD_DIM
-    pick = (pick == lax.broadcasted_iota(jnp.int32, (128, features), 0)).astype(jnp.bfloat16)
-    tail = cols - l_l.shape[1]
-    has_left, has_right = flags[0] > 0, flags[1] > 0
-
-    def lay(value, ahead, fill):
-        blank = jnp.full((tail, value.shape[1]), fill, jnp.float32)
-        return jnp.concatenate([blank, value] if ahead else [value, blank], axis=0)
-
-    def whole(ref, slot, there):
-        value = jnp.concatenate([ref[g, slot].astype(jnp.float32) for g in range(groups)], axis=1)
-        return jnp.where(there, value, 0.0)
-
-    first, second, third = [], [], []
-    mine, lefts, rights = [], [], []
-    for i in range(rows):
-        slot = slots[step * rows + i]
-        a = l_o[slot]
-        b = jnp.where(has_left, lay(l_l[slot], False, NEG), NEG)
-        c = jnp.where(has_right, lay(l_r[slot], True, NEG), NEG)
-        top = jnp.maximum(jnp.maximum(a, b), c)
-        a, b, c = jnp.exp(a - top), jnp.exp(b - top), jnp.exp(c - top)
-        total = a + b + c
-        first.append(a / total)
-        second.append(b / total)
-        third.append(c / total)
-        mine.append(own[slot].astype(jnp.float32))
-        lefts.append(lay(whole(left, slot, has_left), False, 0.0))
-        rights.append(lay(whole(right, slot, has_right), True, 0.0))
-
-    def wide(parts):
-        value = jnp.concatenate(parts, axis=0)
-        high = value.astype(jnp.bfloat16)
-        low = (value - high.astype(jnp.float32)).astype(jnp.bfloat16)
-        dot = lambda x: jnp.dot(x, pick, preferred_element_type=jnp.float32)
-        return dot(high) + dot(low)
-
-    total = wide(first) * jnp.concatenate(mine, axis=0)
-    total = total + wide(second) * jnp.concatenate(lefts, axis=0)
-    total = total + wide(third) * jnp.concatenate(rights, axis=0)
-    attended = total.astype(jnp.bfloat16)
-    a_ref[...] = attended
-    part_ref[...] = jnp.dot(attended, w_ref[...], preferred_element_type=jnp.float32).astype(jnp.bfloat16)
-
-
-def merge(peer, slots, flags, arrays, weight, depth):
-    own = arrays[0]
-    cols, features = own.shape[1:]
-    rows = 4
-    half = weight.shape[1] // 2
-    full = lambda arr: pl.BlockSpec(arr.shape, lambda i, *_: (0,) * arr.ndim)
-    flat = lambda n: pl.BlockSpec((rows * cols, n), lambda i, *_: (i, 0))
-    return pl.pallas_call(
-        merge_kernel,
-        grid_spec=pltpu.PrefetchScalarGridSpec(
-            num_scalar_prefetch=3,
-            grid=(depth // rows,),
-            in_specs=[full(arr) for arr in arrays]
-            + [pl.BlockSpec((features, half), lambda i, p, *_: (0, p[0]))],
-            out_specs=[flat(features), flat(half)],
-        ),
-        out_shape=[
-            jax.ShapeDtypeStruct((depth * cols, features), jnp.bfloat16),
-            jax.ShapeDtypeStruct((depth * cols, half), jnp.bfloat16),
-        ],
-        compiler_params=pltpu.CompilerParams(vmem_limit_bytes=56 * 2**20),
-        cost_estimate=pl.CostEstimate(flops=3 * 10**9, bytes_accessed=2 * 10**7, transcendentals=0),
-        name="merge_project",
-    )(peer, slots, flags, *arrays, weight)
+    )(tiny, slots, q, k, v, *flats, weight)
 
 
 def shards(query_map, key_map, value_map, window_mask, tile_radius, dilation_per_tile, rel_bias, out_weight):
@@ -415,25 +461,14 @@
         dilations.append(jnp.maximum(values[-1], 1))
         wide.append(spread_bias(pattern, values[-2], rel_bias, first, last))
     tiny = jnp.stack(dilations).astype(jnp.int32)
-    arrays = window_attention(tiny, total_rows, query_map, key_map, value_map, wide)
-    o_own, l_own, back_l, back_r, lse_l, lse_r = arrays
     d = dilations[0]
     index = jnp.arange(depth, dtype=jnp.int32)
     turn = index // d
     slots = (d * (turn // BLOCK_ROWS) + index % d) * BLOCK_ROWS + turn % BLOCK_ROWS
-    col = lax.axis_index("col")
-    head = lax.axis_index("head")
-    flags = jnp.stack([col > 0, col < lax.axis_size("col") - 1]).astype(jnp.int32)
-    attended, theirs = merge(
-        (1 - head).astype(jnp.int32).reshape(1), slots.astype(jnp.int32), flags,
-        (o_own, back_l, back_r, l_own, lse_l, lse_r), out_weight, depth,
-    )
-    arrived = lax.ppermute(theirs, "head", [(0, 1), (1, 0)])
-    half = out_weight.shape[1] // 2
-    my_weight = lax.dynamic_slice_in_dim(out_weight, head * half, half, 1)
-    mine = jnp.dot(attended, my_weight, preferred_element_type=jnp.float32)
-    mine, arrived = lax.optimization_barrier((mine, arrived))
-    return (mine + arrived.astype(jnp.float32)).astype(jnp.bfloat16).reshape(depth, cols, half)
+    out = window_attention(
+        tiny, slots.astype(jnp.int32), total_rows, query_map, key_map, value_map, wide, out_weight
+    )
+    return out.reshape(depth, cols, out.shape[2])
 
 
 def solution(mesh):

time: 150 us -> 137 us (0.913)
  waiting for transfers between devices: 29.7 us -> 0.01 us
  Pallas kernels: 87.3 us -> 115 us
  matrix products: 10.7 us -> 0 us
  local copies, waits for them, and re-layouts: 2.35 us -> 7.51 us
  starting transfers between devices: 8.82 us -> 5.84 us
  other arithmetic: 7.75 us -> 5.29 us
    pallas_call x1, Pallas kernels: 75.8 us -> 115 us  [window_attention(): pl.pallas_call(functools.partial(window_kernel, total_rows, groups), in_s...]
    ppermute x1 -> x0, waiting for transfers between devices: 29.7 us -> none  [shards(): arrived = lax.ppermute(theirs, 'head', [(0, 1), (1, 0)])]
    pallas_call x1 -> x0, Pallas kernels: 11.5 us -> none  [merge(): pl.pallas_call(merge_kernel, grid_spec=pltpu.PrefetchScalarGridSpec(num_s...]
    dot_general x4 -> x0, matrix products: 10.7 us -> none  [the longest x3 5.74 us: spread_bias(): wide = jnp.dot(flat, spread, precision=lax.Precision.HIGHEST)]
    unnamed x0 -> x4, local copies, waits for them, and re-layouts: none -> 3.25 us
    ppermute x1 -> x0, starting transfers between devices: 2.98 us -> none  [shards(): arrived = lax.ppermute(theirs, 'head', [(0, 1), (1, 0)])]
    convert_element_type x2 -> x0, other arithmetic: 2.37 us -> none  [the longest x1 1.72 us: shards(): (mine + arrived.astype(jnp.float32)).astype(jnp.bfloat16)]
    pad x0 -> x3, local copies, waits for them, and re-layouts: none -> 2.29 us  [spread_bias(): flat = jnp.pad(flat, ((0, 0), (0, -count % 8), (0, 0)), constant_values=NEG)]
  transfers between devices with their start and end apart: 3 -> 2, of which waited for: 1 -> 0; matrix products, arithmetic and copies ran while one was open for 6% -> 2% of each run, Pallas kernels for 0% -> 0%
where the time goes in v1:
time: 137 us; the launch traced here: 136 us
  Pallas kernels  115 us (84%)
  local copies, waits for them, and re-layouts  7.51 us (5%)
  starting transfers between devices  5.84 us (4%)
  other arithmetic  5.29 us (4%)
  between operations  2.85 us (2%)
    pallas_call x1, Pallas kernels, window_attention(): pl.pallas_call(functools.partial(window_kernel, total_rows, groups), in_s...  115 us
    ppermute x2, starting transfers between devices, shifted(): lax.ppermute(value, axis, [(source, source + steps) for source in range(l...  5.84 us
    unnamed x4, local copies, waits for them, and re-layouts  3.25 us
  transfers between devices with their start and end apart: 2, of which 0 were waited for; matrix products, arithmetic and copies ran while one was open for 2% of the time, Pallas kernels for 0%

profile of v1, /device:TPU:40, one launch (start us, length us, event | category | flops | bytes accessed | tf_op | source)
XLA Modules:
  0.0 136.5 jit_solution(18308367768981460511)
XLA Ops:
  1.3 0.7 reduce
  2.0 0.1 reshape.266
  2.1 0.1 pad_add_fusion
  2.2 2.4 %collective-permute-start.1 = (s32[171]{0:T(256)S(1)}, s32[171]{0:T(256)S(1)}, u32[]{:S(2)}, u32[]{:S(2)}) collective-permute-start(s32[171]{0:T(256)S(1)} %pad_add_fusion), channel_id=1, source_target_pairs={{2,0},{4,2},{6,4},{3,1},{5,3},{7,5},{10,8},{12,10},{14,12},{11,9},... | collective-permute-start | bytes 2060 | tf_op jit(solution)/shard_map/ppermute | solution.py:30
  4.5 3.5 %collective-permute-start = (s32[171]{0:T(256)S(1)}, s32[171]{0:T(256)S(1)}, u32[]{:S(2)}, u32[]{:S(2)}) collective-permute-start(s32[171]{0:T(256)S(1)} %pad_add_fusion), channel_id=1, source_target_pairs={{0,2},{2,4},{4,6},{1,3},{3,5},{5,7},{8,10},{10,12},{12,14},{9,11},... | collective-permute-start | bytes 2060 | tf_op jit(solution)/shard_map/ppermute | solution.py:30
  8.0 0.7 broadcast_compare_fusion
  8.8 0.7 fusion.13.slots
  9.5 0.0 collective-permute-done.1
  9.5 0.7 fusion.14
  10.2 0.7 broadcast_compare_fusion.1
  10.8 0.1 eq.65
  11.6 0.0 collective-permute-done
  11.6 0.7 fusion.15
  12.9 0.7 broadcast_compare_fusion.2
  13.6 0.1 eq.63
  13.7 0.1 fusion.11
  13.8 0.1 copy.15
  13.9 0.1 copy.12
  14.0 0.1 copy.9
  14.1 1.0 select_bitcast_fusion
  15.3 0.2 copy.21
  15.5 0.2 copy.20
  15.6 0.8 pad.27.clone
  16.4 0.7 pad.25.clone
  17.2 0.2 copy.19
  17.4 0.8 pad.23.clone
  18.2 0.6 pad_add_fusion.1.tiny
  18.8 115.0 %window_attention.1 = bf16[4,128,1536]{2,1,0:T(8,128)(2,1)} custom-call(s32[3]{0:T(128)} %pad_add_fusion.1.tiny, s32[16]{0:T(128)} %fusion.13.slots, bf16[16,32,1536]{2,1,0:T(8,128)(2,1)} %q_ref.1, bf16[16,32,1536]{2,1,0:T(8,128)(2,1)} %k_own.1, bf16[16,32,1536]{2,1,0:T(8,128)(2,1)} %v_own.1, f32[960,16]{1,0:T(8,128)} %bitcast.47, f32[576,16]{1,0:T(8,128)} %bitcast.49, ...), custom_call_target="tpu_custom_call" | custom-call | flops 20000000000 | bytes 40000000 | tf_op jit(solution)/shard_map/window_attention/pallas_call | solution.py:407
  133.8 2.7 %copy.29 = bf16[16,32,1536]{2,1,0:T(8,128)(2,1)} copy(bf16[16,32,1536]{2,1,0:T(8,128)(2,1)} %bitcast.43) | data formatting | bytes 3145728
  (11 shorter events, 0.2 us)
Async XLA Ops:
  2.2 7.3 %collective-permute-start.1 = (s32[171]{0:T(256)S(1)}, s32[171]{0:T(256)S(1)}, u32[]{:S(2)}, u32[]{:S(2)}) collective-permute-start(s32[171]{0:T(256)S(1)} %pad_add_fusion), channel_id=1, source_target_pairs={{2,0},{4,2},{6,4},{3,1},{5,3},{7,5},{10,8},{12,10},{14,12},{11,9},... | collective-permute-start | bytes 2060 | tf_op jit(solution)/shard_map/ppermute | solution.py:30
  4.5 7.1 %collective-permute-start = (s32[171]{0:T(256)S(1)}, s32[171]{0:T(256)S(1)}, u32[]{:S(2)}, u32[]{:S(2)}) collective-permute-start(s32[171]{0:T(256)S(1)} %pad_add_fusion), channel_id=1, source_target_pairs={{0,2},{2,4},{4,6},{1,3},{3,5},{5,7},{8,10},{10,12},{12,14},{9,11},... | collective-permute-start | bytes 2060 | tf_op jit(solution)/shard_map/ppermute | solution.py:30

commit v2 on v1

--- a/solution.py
+++ b/solution.py
@@ -30,25 +30,18 @@
     return lax.ppermute(value, axis, [(source, source + steps) for source in range(leading, last)])
 
 
-def spread_bias(pattern, radius, rel_bias, first, last):
-    heads = rel_bias.shape[0]
-    steps = jnp.abs(jnp.arange(WINDOW, dtype=jnp.int32) - RADIUS_MAX)
-    centre = (steps[:, None] == 0) & (steps[None, :] == 0)
-    near = (steps[:, None] <= radius) & (steps[None, :] <= radius)
-    used = ((pattern == 1) | centre) & near
-    masked = jnp.where(used[None], rel_bias, NEG)
-    turned = jnp.swapaxes(masked, 1, 2)[:, first:last]
+def block_form(value, first, last, fill):
+    turned = jnp.swapaxes(value, 1, 2)[:, first:last]
     extra = BLOCK_KEYS - WINDOW
-    turned = jnp.pad(turned, ((0, 0), (0, 0), (BLOCK_ROWS - 1, extra)), constant_values=NEG)
+    turned = jnp.pad(turned, ((0, 0), (0, 0), (BLOCK_ROWS - 1, extra)), constant_values=fill)
     parts = [turned[:, :, BLOCK_ROWS - 1 - t :][:, :, :BLOCK_KEYS] for t in range(BLOCK_ROWS)]
     count = BLOCK_ROWS * (last - first)
-    flat = jnp.stack(parts, axis=1).reshape(heads, count, BLOCK_KEYS)
-    flat = jnp.pad(flat, ((0, 0), (0, -count % 8), (0, 0)), constant_values=NEG)
-    return flat.reshape(-1, BLOCK_KEYS)
-
-
-def expand_bias(flat_ref, x_ref):
-    value = flat_ref[...]
+    flat = jnp.stack(parts, axis=1).reshape(value.shape[0], count, BLOCK_KEYS)
+    return jnp.pad(flat, ((0, 0), (0, -count % 8), (0, 0)), constant_values=fill)
+
+
+def expand_bias(flat_ref, mask_ref, x_ref):
+    value = (flat_ref[...] + mask_ref[...][None]).reshape(x_ref.shape[0], BLOCK_KEYS)
     high = value.astype(jnp.bfloat16)
     rest = value - high.astype(jnp.float32)
     middle = rest.astype(jnp.bfloat16)
@@ -87,7 +80,7 @@
     return jnp.where(d == 1, 3 * beta, jnp.where(d == 2, two, three))
 
 
-def one_set(d, row_anchor, total_rows, group, beta, load_q, t_ref, store_o, l_ref, k_ref, v_ref, s_ref, p_ref):
+def one_set(d, row_anchor, total_rows, group, beta, load_q, t_ref, store_o, load_l, store_l, k_ref, v_ref, s_ref, p_ref):
     cols = t_ref.shape[2]
     base = base_row(beta, d)
     span = k_ref.shape[0]
@@ -132,7 +125,7 @@
     for t in range(BLOCK_ROWS):
         slot = beta * BLOCK_ROWS + t
         out = jnp.zeros((cols, LANES), jnp.float32)
-        stats = l_ref[slot]
+        stats, lane0 = load_l(slot)
         for h in range(GROUP):
             at = h * BLOCK_ROWS + t
             total = sums[at]
@@ -140,9 +133,9 @@
             inverse = 1.0 / jnp.where(some, total, 1.0)
             out = jnp.where(head_of == h, mixed[at * cols : (at + 1) * cols] * inverse, out)
             lse = jnp.where(some, peaks[at] + jnp.log(jnp.where(some, total, 1.0)), NEG)
-            stats = jnp.where(stat_lane == group * GROUP + h, lse, stats)
+            stats = jnp.where(stat_lane == lane0 + h, lse, stats)
         store_o(slot, out.astype(jnp.bfloat16))
-        l_ref[slot] = stats
+        store_l(slot, stats)
 
 
 def merge_rows(step, rows, slots, has_left, has_right, own, left, right, l_o, l_l, l_r):
@@ -152,6 +145,16 @@
     pick = (pick == lax.broadcasted_iota(jnp.int32, (128, features), 0)).astype(jnp.bfloat16)
     tail = cols - l_l.shape[1]
 
+    def found(ref, slot):
+        lane = lax.broadcasted_iota(jnp.int32, (cols - tail, 128), 1)
+        value = jnp.full((cols - tail, 128), NEG, jnp.float32)
+        for g in range(groups):
+            packed = ref[g]
+            for h in range(GROUP):
+                one = jnp.sum(jnp.where(lane == slot * GROUP + h, packed, 0.0), axis=1, keepdims=True)
+                value = jnp.where(lane == g * GROUP + h, one, value)
+        return value
+
     def lay(value, ahead, fill):
         blank = jnp.full((tail, value.shape[1]), fill, jnp.float32)
         return jnp.concatenate([blank, value] if ahead else [value, blank], axis=0)
@@ -165,8 +168,8 @@
     for i in range(rows):
         slot = slots[step * rows + i]
         a = l_o[slot]
-        b = jnp.where(has_left, lay(l_l[slot], False, NEG), NEG)
-        c = jnp.where(has_right, lay(l_r[slot], True, NEG), NEG)
+        b = jnp.where(has_left, lay(found(l_l, slot), False, NEG), NEG)
+        c = jnp.where(has_right, lay(found(l_r, slot), True, NEG), NEG)
         top = jnp.maximum(jnp.maximum(a, b), c)
         a, b, c = jnp.exp(a - top), jnp.exp(b - top), jnp.exp(c - top)
         total = a + b + c
@@ -191,12 +194,12 @@
 
 
 def window_kernel(
-    total_rows, groups, tiny, slots, q_ref, k_own, v_own, flat_o, flat_l, flat_r, w_hbm,
+    total_rows, groups, d_own, slots, q_ref, k_own, v_own, flat_o, flat_l, flat_r, m_o, m_right, m_left, w_hbm,
     result,
     o_own, l_own, back_l, back_r, lse_l, lse_r, w_theirs, w_mine, attended, parts, arrived, x_o, x_l, x_r,
     win_k, win_v, k_ref, v_ref, land_l, land_r, q_l, q_r, t_o, t_l, t_r,
     s_o, s_l, s_r, p_o, p_l, p_r, out_l, out_r, st_l, st_r,
-    send, recv, back_send, back_recv, head_send, head_recv, w_sem,
+    send, recv, back_send, back_recv, head_send, head_recv, w_sem, m_l, m_r, d_l, d_r, set_send, set_recv,
 ):
     row, col, head = lax.axis_index("row"), lax.axis_index("col"), lax.axis_index("head")
     rows, cols_n = lax.axis_size("row"), lax.axis_size("col")
@@ -219,10 +222,13 @@
         def _():
             for ref in (win_k, win_v):
                 ref[:, at : at + n] = jnp.zeros((groups, n, cols, LANES), ref.dtype)
-    for edge, ref in ((col < 1, land_l), (col > cols_n - 2, land_r)):
+    for edge, ref, mask, d_ref in ((col < 1, land_l, m_l, d_l), (col > cols_n - 2, land_r, m_r, d_r)):
         @pl.when(edge)
         def _():
             ref[...] = jnp.zeros_like(ref)
+            mask[...] = jnp.full(mask.shape, NEG, jnp.float32)
+            for n in range(d_ref.shape[0]):
+                d_ref[n] = 1
 
     peers = (
         (row < rows - 1, {"row": row + 1}),
@@ -266,23 +272,37 @@
             )))
         return made
 
-    def backs(g):
+    per = SLOTS // 2
+
+    def backs(k):
+        g, at = k // 2, pl.ds((k % 2) * per, per)
         made = []
         for n, (to, frm, src, dst) in enumerate(((5, 4, out_l, back_r), (4, 5, out_r, back_l))):
             there, peer = peers[to]
             made.append((there, peers[frm][0], pltpu.make_async_remote_copy(
-                src_ref=src.at[g], dst_ref=dst.at[g], send_sem=back_send.at[g, n],
-                recv_sem=back_recv.at[g, n], device_id=peer, device_id_type=MESH,
+                src_ref=src.at[g, at], dst_ref=dst.at[g, at], send_sem=back_send.at[k, n],
+                recv_sem=back_recv.at[k, n], device_id=peer, device_id_type=MESH,
             )))
         return made
 
-    def lses():
+    def lses(g):
         made = []
         for n, (to, frm, src, dst) in enumerate(((5, 4, st_l, lse_r), (4, 5, st_r, lse_l))):
             there, peer = peers[to]
             made.append((there, peers[frm][0], pltpu.make_async_remote_copy(
-                src_ref=src, dst_ref=dst, send_sem=back_send.at[groups, n],
-                recv_sem=back_recv.at[groups, n], device_id=peer, device_id_type=MESH,
+                src_ref=src.at[g], dst_ref=dst.at[g], send_sem=back_send.at[2 * groups + g, n],
+                recv_sem=back_recv.at[2 * groups + g, n], device_id=peer, device_id_type=MESH,
+            )))
+        return made
+
+    def settings():
+        made = []
+        plan = ((4, 5, m_right, m_l), (4, 5, d_own, d_l), (5, 4, m_left, m_r), (5, 4, d_own, d_r))
+        for n, (to, frm, src, dst) in enumerate(plan):
+            there, peer = peers[to]
+            made.append((there, peers[frm][0], pltpu.make_async_remote_copy(
+                src_ref=src, dst_ref=dst, send_sem=set_send.at[n], recv_sem=set_recv.at[n],
+                device_id=peer, device_id_type=MESH,
             )))
         return made
 
@@ -292,35 +312,47 @@
             def _():
                 act(entry[2])
 
+    each(settings(), 0, lambda copy: copy.start())
+
     @pl.loop(0, groups)
     def _(g):
         each(copies(g), 0, lambda copy: copy.start())
 
     for copy in weights:
         copy.start()
-    for flat, wide in ((flat_o, x_o), (flat_l, x_l), (flat_r, x_r)):
-        expand_bias(flat, wide)
-    fill_table(0, 0, WINDOW, tiny[0], x_o, t_o)
-    fill_table(side, RADIUS_MAX + 1, WINDOW, tiny[1], x_l, t_l)
-    fill_table(-cols, 0, RADIUS_MAX, tiny[2], x_r, t_r)
+    expand_bias(flat_o, m_o, x_o)
+    fill_table(0, 0, WINDOW, d_own[0], x_o, t_o)
+    each(settings(), 1, lambda copy: copy.wait_recv())
+    expand_bias(flat_l, m_l, x_l)
+    expand_bias(flat_r, m_r, x_r)
+    fill_table(side, RADIUS_MAX + 1, WINDOW, d_l[0], x_l, t_l)
+    fill_table(-cols, 0, RADIUS_MAX, d_r[0], x_r, t_r)
     for ref in (l_own, st_l, st_r):
         ref[...] = jnp.zeros_like(ref)
     anchor = row * depth
 
-    @pl.loop(0, groups)
-    def _(g):
+    @pl.loop(0, 2 * groups)
+    def _(k):
+        g, part = k // 2, k % 2
         at = pl.ds(pl.multiple_of(g * LANES, LANES), LANES)
-        each(copies(g), 1, lambda copy: copy.wait_recv())
-        for ref, win, own in ((k_ref, win_k, k_own), (v_ref, win_v, v_own)):
-            ref[0:HALO] = win[g, 0:HALO]
-            ref[HALO : HALO + depth] = own[:, :, at]
-            ref[HALO + depth : 2 * HALO + depth] = win[g, HALO : 2 * HALO]
-        q_l[...] = land_l[g]
-        q_r[...] = land_r[g]
-
-        @pl.when(g > 0)
-        def _():
-            each(backs(g - 1), 0, lambda copy: copy.start())
+
+        @pl.when(part == 0)
+        def _():
+            each(copies(g), 1, lambda copy: copy.wait_recv())
+            for ref, win, own in ((k_ref, win_k, k_own), (v_ref, win_v, v_own)):
+                ref[0:HALO] = win[g, 0:HALO]
+                ref[HALO : HALO + depth] = own[:, :, at]
+                ref[HALO + depth : 2 * HALO + depth] = win[g, HALO : 2 * HALO]
+            q_l[...] = land_l[g]
+            q_r[...] = land_r[g]
+
+        @pl.when(k > 0)
+        def _():
+            each(backs(k - 1), 0, lambda copy: copy.start())
+
+        @pl.when((k > 0) & (part == 0))
+        def _():
+            each(lses(g - 1), 0, lambda copy: copy.start())
 
         def put_own(slot, value):
             o_own[slot, :, at] = value
@@ -331,27 +363,38 @@
         def put_right(slot, value):
             out_r[g, slot] = value
 
-        @pl.loop(0, BLOCKS)
-        def _(beta):
-            one_set(tiny[0], anchor, total_rows, g, beta, lambda i: q_ref[i, :, at], t_o, put_own, l_own, k_ref, v_ref, s_o, p_o)
-            one_set(tiny[1], anchor, total_rows, g, beta, lambda i: q_l[i], t_l, put_left, st_l, k_ref, v_ref, s_l, p_l)
-            one_set(tiny[2], anchor, total_rows, g, beta, lambda i: q_r[i], t_r, put_right, st_r, k_ref, v_ref, s_r, p_r)
+        def put_l_own(slot, value):
+            l_own[slot] = value
+
+        def put_l_left(slot, value):
+            st_l[g] = value
+
+        def put_l_right(slot, value):
+            st_r[g] = value
+
+        @pl.loop(0, BLOCKS // 2)
+        def _(i):
+            beta = part * (BLOCKS // 2) + i
+            one_set(d_own[0], anchor, total_rows, g, beta, lambda i: q_ref[i, :, at], t_o, put_own, lambda slot: (l_own[slot], g * GROUP), put_l_own, k_ref, v_ref, s_o, p_o)
+            one_set(d_l[0], anchor, total_rows, g, beta, lambda i: q_l[i], t_l, put_left, lambda slot: (st_l[g], slot * GROUP), put_l_left, k_ref, v_ref, s_l, p_l)
+            one_set(d_r[0], anchor, total_rows, g, beta, lambda i: q_r[i], t_r, put_right, lambda slot: (st_r[g], slot * GROUP), put_l_right, k_ref, v_ref, s_r, p_r)
 
     for copy in weights:
         copy.wait()
+    each(settings(), 0, lambda copy: copy.wait_send())
 
     @pl.loop(0, groups)
     def _(g):
         each(copies(g), 0, lambda copy: copy.wait_send())
 
-    each(backs(groups - 1), 0, lambda copy: copy.start())
-    each(lses(), 0, lambda copy: copy.start())
+    each(backs(2 * groups - 1), 0, lambda copy: copy.start())
+    each(lses(groups - 1), 0, lambda copy: copy.start())
 
     @pl.loop(0, groups)
     def _(g):
-        each(backs(g), 1, lambda copy: copy.wait_recv())
-
-    each(lses(), 1, lambda copy: copy.wait_recv())
+        each(backs(2 * g), 1, lambda copy: copy.wait_recv())
+        each(backs(2 * g + 1), 1, lambda copy: copy.wait_recv())
+        each(lses(g), 1, lambda copy: copy.wait_recv())
 
     def swap(i):
         return pltpu.make_async_remote_copy(
@@ -375,9 +418,10 @@
 
     @pl.loop(0, groups)
     def _(g):
-        each(backs(g), 0, lambda copy: copy.wait_send())
-
-    each(lses(), 0, lambda copy: copy.wait_send())
+        each(backs(2 * g), 0, lambda copy: copy.wait_send())
+        each(backs(2 * g + 1), 0, lambda copy: copy.wait_send())
+        each(lses(g), 0, lambda copy: copy.wait_send())
+
     swap(steps - 1).start()
 
     @pl.loop(0, steps)
@@ -391,7 +435,7 @@
         swap(i).wait_send()
 
 
-def window_attention(tiny, slots, total_rows, q, k, v, flats, weight):
+def window_attention(dilation, slots, total_rows, q, k, v, flats, masks, weight):
     depth, cols, features = q.shape
     groups = features // LANES
     heads = groups * GROUP
@@ -406,7 +450,7 @@
     dma = pltpu.SemaphoreType.DMA
     return pl.pallas_call(
         functools.partial(window_kernel, total_rows, groups),
-        in_specs=[smem, smem] + [vmem] * 6 + [pl.BlockSpec(memory_space=pl.ANY)],
+        in_specs=[smem, smem] + [vmem] * 9 + [pl.BlockSpec(memory_space=pl.ANY)],
         out_specs=vmem,
         out_shape=jax.ShapeDtypeStruct((steps, tokens, half), bf16),
         scratch_shapes=[
@@ -414,15 +458,15 @@
             pltpu.VMEM((SLOTS, cols, 128), f32),
             pltpu.VMEM((groups, SLOTS, SIDE_COLS, LANES), bf16),
             pltpu.VMEM((groups, SLOTS, SIDE_COLS, LANES), bf16),
-            pltpu.VMEM((SLOTS, SIDE_COLS, 128), f32),
-            pltpu.VMEM((SLOTS, SIDE_COLS, 128), f32),
+            pltpu.VMEM((groups, SIDE_COLS, 128), f32),
+            pltpu.VMEM((groups, SIDE_COLS, 128), f32),
             pltpu.VMEM((features, half), bf16),
             pltpu.VMEM((features, half), bf16),
             pltpu.VMEM((steps, tokens, features), bf16),
             pltpu.VMEM((steps, tokens, half), bf16),
             pltpu.VMEM((steps, tokens, half), bf16),
         ]
-        + [pltpu.VMEM((flat.shape[0], keys), f32) for flat in flats]
+        + [pltpu.VMEM((flat.shape[0] * flat.shape[1], keys), f32) for flat in flats]
         + [pltpu.VMEM((groups, 2 * HALO, cols, LANES), bf16)] * 2
         + [pltpu.VMEM((depth + 2 * HALO, cols, LANES), bf16)] * 2
         + [pltpu.VMEM((groups, depth, SIDE_COLS, LANES), bf16)] * 2
@@ -431,42 +475,39 @@
         + [pltpu.VMEM((GROUP * BLOCK_ROWS * n, keys), f32) for n in counts]
         + [pltpu.VMEM((GROUP * BLOCK_ROWS * n, keys), bf16) for n in counts]
         + [pltpu.VMEM((groups, SLOTS, SIDE_COLS, LANES), bf16)] * 2
-        + [pltpu.VMEM((SLOTS, SIDE_COLS, 128), f32)] * 2
-        + [dma((groups, 10)), dma((groups, 10)), dma((groups + 1, 2)), dma((groups + 1, 2))]
-        + [dma((steps,)), dma((steps,)), dma((2,))],
+        + [pltpu.VMEM((groups, SIDE_COLS, 128), f32)] * 2
+        + [dma((groups, 10)), dma((groups, 10)), dma((3 * groups, 2)), dma((3 * groups, 2))]
+        + [dma((steps,)), dma((steps,)), dma((2,))]
+        + [pltpu.VMEM(masks[1].shape, f32), pltpu.VMEM(masks[2].shape, f32)]
+        + [pltpu.SMEM(dilation.shape, jnp.int32)] * 2
+        + [dma((4,)), dma((4,))],
         compiler_params=pltpu.CompilerParams(
             collective_id=0, has_side_effects=True, vmem_limit_bytes=67_000_000
         ),
         cost_estimate=pl.CostEstimate(flops=2 * 10**10, bytes_accessed=4 * 10**7, transcendentals=0),
         name="window_attention",
-    )(tiny, slots, q, k, v, *flats, weight)
+    )(dilation, slots, q, k, v, *flats, *masks, weight)
 
 
 def shards(query_map, key_map, value_map, window_mask, tile_radius, dilation_per_tile, rel_bias, out_weight):
     depth, cols, features = query_map.shape
     total_rows = depth * lax.axis_size("row")
-    settings = jnp.concatenate(
-        [window_mask.reshape(-1), tile_radius.reshape(-1), dilation_per_tile.reshape(-1)]
-    )
-    from_left = shifted(settings, "col", 1)
-    from_right = shifted(settings, "col", -1)
-    wide = []
-    dilations = []
-    for values, first, last in (
-        (settings, 0, WINDOW),
-        (from_left, RADIUS_MAX + 1, WINDOW),
-        (from_right, 0, RADIUS_MAX),
-    ):
-        pattern = values[:-2].reshape(WINDOW, WINDOW)
-        dilations.append(jnp.maximum(values[-1], 1))
-        wide.append(spread_bias(pattern, values[-2], rel_bias, first, last))
-    tiny = jnp.stack(dilations).astype(jnp.int32)
-    d = dilations[0]
+    steps = jnp.abs(jnp.arange(WINDOW, dtype=jnp.int32) - RADIUS_MAX)
+    centre = (steps[:, None] == 0) & (steps[None, :] == 0)
+    radius = tile_radius[0, 0]
+    near = (steps[:, None] <= radius) & (steps[None, :] <= radius)
+    used = ((window_mask[0, 0] == 1) | centre) & near
+    used = jnp.where(used, 0.0, NEG).astype(jnp.float32)[None]
+    spans = ((0, WINDOW), (RADIUS_MAX + 1, WINDOW), (0, RADIUS_MAX))
+    flats = [block_form(rel_bias, *span, NEG) for span in spans]
+    masks = [block_form(used, *span, NEG)[0] for span in spans]
+    d = dilation_per_tile[0, 0]
     index = jnp.arange(depth, dtype=jnp.int32)
     turn = index // d
     slots = (d * (turn // BLOCK_ROWS) + index % d) * BLOCK_ROWS + turn % BLOCK_ROWS
     out = window_attention(
-        tiny, slots.astype(jnp.int32), total_rows, query_map, key_map, value_map, wide, out_weight
+        jnp.full((16,), d, jnp.int32), slots.astype(jnp.int32), total_rows,
+        query_map, key_map, value_map, flats, masks, out_weight,
     )
     return out.reshape(depth, cols, out.shape[2])
 

time: 137 us -> 124 us (0.905)
  starting transfers between devices: 5.84 us -> 0 us
  Pallas kernels: 115 us -> 111 us
  other arithmetic: 5.29 us -> 1.55 us
  local copies, waits for them, and re-layouts: 7.51 us -> 9.55 us
  between operations: 2.85 us -> 1.41 us
    ppermute x2 -> x0, starting transfers between devices: 5.84 us -> none  [shifted(): lax.ppermute(value, axis, [(source, source + steps) for source in range(l...]
    pallas_call x1, Pallas kernels: 115 us -> 111 us  [window_attention(): pl.pallas_call(functools.partial(window_kernel, total_rows, groups), in_s...]
    squeeze x0 -> x3, local copies, waits for them, and re-layouts: none -> 1.82 us  [shards(): masks = [block_form(used, *span, NEG)[0] for span in spans]]
    unnamed x4 -> x2, local copies, waits for them, and re-layouts: 3.25 us -> 3.62 us
  transfers between devices with their start and end apart: 2 -> 0, of which waited for: 0 -> 0; matrix products, arithmetic and copies ran while one was open for 2% -> 0% of each run, Pallas kernels for 0% -> 0%
where the time goes in v2:
time: 124 us; the launch traced here: 123 us
  Pallas kernels  111 us (90%)
  local copies, waits for them, and re-layouts  9.55 us (8%)
  other arithmetic  1.55 us (1%)
  between operations  1.41 us (1%)
    pallas_call x1, Pallas kernels, window_attention(): pl.pallas_call(functools.partial(window_kernel, total_rows, groups), in_s...  111 us
    unnamed x2, local copies, waits for them, and re-layouts  3.62 us

profile of v2, /device:TPU:40, one launch (start us, length us, event | category | flops | bytes accessed | tf_op | source)
XLA Modules:
  0.0 123.3 jit_solution(9426472225008814469)
XLA Ops:
  1.3 0.7 fusion.13.slots
  2.0 0.5 broadcast_in_dim.16.d_own
  2.5 0.7 broadcast_compare_fusion
  3.2 0.1 select_bitcast_fusion
  3.3 0.1 fusion.18
  3.3 0.1 copy.29
  3.4 0.1 copy.30
  3.5 0.1 copy.31
  3.6 0.6 pad_bitcast_fusion.1.m_left
  4.2 0.1 copy.23
  4.3 0.6 pad_bitcast_fusion.m_o
  5.0 0.1 copy.25
  5.0 0.1 copy.26
  5.1 0.1 copy.27
  5.2 0.6 pad_bitcast_fusion.2.m_right
  5.8 0.9 copy.36
  6.8 0.2 copy.21
  7.0 0.7 pad.47.flat_l
  7.8 0.2 copy.22
  7.9 0.8 pad.49.flat_r
  8.7 0.2 copy.20
  9.0 0.8 pad.45.flat_o
  9.8 110.8 %window_attention.1 = bf16[4,128,1536]{2,1,0:T(8,128)(2,1)} custom-call(s32[16]{0:T(128)} %broadcast_in_dim.16.d_own, s32[16]{0:T(128)} %fusion.13.slots, bf16[16,32,1536]{2,1,0:T(8,128)(2,1)} %q_ref.1, bf16[16,32,1536]{2,1,0:T(8,128)(2,1)} %k_own.1, bf16[16,32,1536]{2,1,0:T(8,128)(2,1)} %v_own.1, f32[24,40,16]{2,1,0:T(8,128)} %pad.45.flat_o, ...), custom_call_target="tpu_custom_call" | custom-call | flops 20000000000 | bytes 40000000 | tf_op jit(solution)/shard_map/window_attention/pallas_call | solution.py:451
  120.7 2.7 %copy.40 = bf16[16,32,1536]{2,1,0:T(8,128)(2,1)} copy(bf16[16,32,1536]{2,1,0:T(8,128)(2,1)} %bitcast.62) | data formatting | bytes 3145728
  (16 shorter events, 0.2 us)

commit v3 on v2

--- a/solution.py
+++ b/solution.py
@@ -30,18 +30,18 @@
     return lax.ppermute(value, axis, [(source, source + steps) for source in range(leading, last)])
 
 
-def block_form(value, first, last, fill):
-    turned = jnp.swapaxes(value, 1, 2)[:, first:last]
+def block_form(value, fill):
+    turned = jnp.swapaxes(value, 1, 2)
     extra = BLOCK_KEYS - WINDOW
-    turned = jnp.pad(turned, ((0, 0), (0, 0), (BLOCK_ROWS - 1, extra)), constant_values=fill)
-    parts = [turned[:, :, BLOCK_ROWS - 1 - t :][:, :, :BLOCK_KEYS] for t in range(BLOCK_ROWS)]
-    count = BLOCK_ROWS * (last - first)
-    flat = jnp.stack(parts, axis=1).reshape(value.shape[0], count, BLOCK_KEYS)
+    count = BLOCK_ROWS * WINDOW
+    parts = [
+        jnp.pad(turned, ((0, 0), (0, 0), (t, extra - t)), constant_values=fill) for t in range(BLOCK_ROWS)
+    ]
+    flat = jnp.concatenate(parts, axis=1)
     return jnp.pad(flat, ((0, 0), (0, -count % 8), (0, 0)), constant_values=fill)
 
 
-def expand_bias(flat_ref, mask_ref, x_ref):
-    value = (flat_ref[...] + mask_ref[...][None]).reshape(x_ref.shape[0], BLOCK_KEYS)
+def expand_bias(value, x_ref):
     high = value.astype(jnp.bfloat16)
     rest = value - high.astype(jnp.float32)
     middle = rest.astype(jnp.bfloat16)
@@ -53,14 +53,14 @@
     x_ref[...] = dot(high) + dot(middle) + dot(low)
 
 
-def fill_table(offset, first, last, d, x_ref, t_ref):
+def fill_table(offset, first, last, d, x_ref, mask_ref, t_ref):
     heads, _, cols, width = t_ref.shape
     stride = x_ref.shape[0] // heads
     count = last - first
 
     @pl.loop(0, heads)
     def _(h):
-        rows = x_ref[pl.ds(pl.multiple_of(h * stride, 8), stride)]
+        rows = x_ref[pl.ds(pl.multiple_of(h * stride, 8), stride)] + mask_ref[...]
         for top in range(0, cols, 8):
             lane = lax.broadcasted_iota(jnp.int32, (8, 128), 1)
             rel = lane % 32 - lax.broadcasted_iota(jnp.int32, (8, 128), 0) + (offset - top)
@@ -69,7 +69,7 @@
                 for left in range(0, width, 128):
                     acc = jnp.full((8, 128), NEG, jnp.float32)
                     for b in range(count):
-                        at = t * count + b
+                        at = t * WINDOW + first + b
                         acc = jnp.where(masks[b], rows[at : at + 1, left : left + 128], acc)
                     t_ref[h, t, top : top + 8, left : left + 128] = acc
 
@@ -194,9 +194,9 @@
 
 
 def window_kernel(
-    total_rows, groups, d_own, slots, q_ref, k_own, v_own, flat_o, flat_l, flat_r, m_o, m_right, m_left, w_hbm,
+    total_rows, groups, d_own, slots, q_ref, k_own, v_own, flat, m_o, w_hbm,
     result,
-    o_own, l_own, back_l, back_r, lse_l, lse_r, w_theirs, w_mine, attended, parts, arrived, x_o, x_l, x_r,
+    o_own, l_own, back_l, back_r, lse_l, lse_r, w_theirs, w_mine, attended, parts, arrived, x_all, xm_o, xm_l, xm_r,
     win_k, win_v, k_ref, v_ref, land_l, land_r, q_l, q_r, t_o, t_l, t_r,
     s_o, s_l, s_r, p_o, p_l, p_r, out_l, out_r, st_l, st_r,
     send, recv, back_send, back_recv, head_send, head_recv, w_sem, m_l, m_r, d_l, d_r, set_send, set_recv,
@@ -297,7 +297,7 @@
 
     def settings():
         made = []
-        plan = ((4, 5, m_right, m_l), (4, 5, d_own, d_l), (5, 4, m_left, m_r), (5, 4, d_own, d_r))
+        plan = ((4, 5, m_o, m_l), (4, 5, d_own, d_l), (5, 4, m_o, m_r), (5, 4, d_own, d_r))
         for n, (to, frm, src, dst) in enumerate(plan):
             there, peer = peers[to]
             made.append((there, peers[frm][0], pltpu.make_async_remote_copy(
@@ -320,13 +320,14 @@
 
     for copy in weights:
         copy.start()
-    expand_bias(flat_o, m_o, x_o)
-    fill_table(0, 0, WINDOW, d_own[0], x_o, t_o)
+    expand_bias(flat[...].reshape(x_all.shape[0], BLOCK_KEYS), x_all)
+    expand_bias(m_o[...], xm_o)
+    fill_table(0, 0, WINDOW, d_own[0], x_all, xm_o, t_o)
     each(settings(), 1, lambda copy: copy.wait_recv())
-    expand_bias(flat_l, m_l, x_l)
-    expand_bias(flat_r, m_r, x_r)
-    fill_table(side, RADIUS_MAX + 1, WINDOW, d_l[0], x_l, t_l)
-    fill_table(-cols, 0, RADIUS_MAX, d_r[0], x_r, t_r)
+    expand_bias(m_l[...], xm_l)
+    expand_bias(m_r[...], xm_r)
+    fill_table(side, RADIUS_MAX + 1, WINDOW, d_l[0], x_all, xm_l, t_l)
+    fill_table(-cols, 0, RADIUS_MAX, d_r[0], x_all, xm_r, t_r)
     for ref in (l_own, st_l, st_r):
         ref[...] = jnp.zeros_like(ref)
     anchor = row * depth
@@ -435,7 +436,7 @@
         swap(i).wait_send()
 
 
-def window_attention(dilation, slots, total_rows, q, k, v, flats, masks, weight):
+def window_attention(dilation, slots, total_rows, q, k, v, flat, mask, weight):
     depth, cols, features = q.shape
     groups = features // LANES
     heads = groups * GROUP
@@ -450,7 +451,7 @@
     dma = pltpu.SemaphoreType.DMA
     return pl.pallas_call(
         functools.partial(window_kernel, total_rows, groups),
-        in_specs=[smem, smem] + [vmem] * 9 + [pl.BlockSpec(memory_space=pl.ANY)],
+        in_specs=[smem, smem] + [vmem] * 5 + [pl.BlockSpec(memory_space=pl.ANY)],
         out_specs=vmem,
         out_shape=jax.ShapeDtypeStruct((steps, tokens, half), bf16),
         scratch_shapes=[
@@ -466,7 +467,8 @@
             pltpu.VMEM((steps, tokens, half), bf16),
             pltpu.VMEM((steps, tokens, half), bf16),
         ]
-        + [pltpu.VMEM((flat.shape[0] * flat.shape[1], keys), f32) for flat in flats]
+        + [pltpu.VMEM((flat.shape[0] * flat.shape[1], keys), f32)]
+        + [pltpu.VMEM((flat.shape[1], keys), f32)] * 3
         + [pltpu.VMEM((groups, 2 * HALO, cols, LANES), bf16)] * 2
         + [pltpu.VMEM((depth + 2 * HALO, cols, LANES), bf16)] * 2
         + [pltpu.VMEM((groups, depth, SIDE_COLS, LANES), bf16)] * 2
@@ -478,7 +480,7 @@
         + [pltpu.VMEM((groups, SIDE_COLS, 128), f32)] * 2
         + [dma((groups, 10)), dma((groups, 10)), dma((3 * groups, 2)), dma((3 * groups, 2))]
         + [dma((steps,)), dma((steps,)), dma((2,))]
-        + [pltpu.VMEM(masks[1].shape, f32), pltpu.VMEM(masks[2].shape, f32)]
+        + [pltpu.VMEM(mask.shape, f32)] * 2
         + [pltpu.SMEM(dilation.shape, jnp.int32)] * 2
         + [dma((4,)), dma((4,))],
         compiler_params=pltpu.CompilerParams(
@@ -486,7 +488,7 @@
         ),
         cost_estimate=pl.CostEstimate(flops=2 * 10**10, bytes_accessed=4 * 10**7, transcendentals=0),
         name="window_attention",
-    )(dilation, slots, q, k, v, *flats, *masks, weight)
+    )(dilation, slots, q, k, v, flat, mask, weight)
 
 
 def shards(query_map, key_map, value_map, window_mask, tile_radius, dilation_per_tile, rel_bias, out_weight):
@@ -498,16 +500,15 @@
     near = (steps[:, None] <= radius) & (steps[None, :] <= radius)
     used = ((window_mask[0, 0] == 1) | centre) & near
     used = jnp.where(used, 0.0, NEG).astype(jnp.float32)[None]
-    spans = ((0, WINDOW), (RADIUS_MAX + 1, WINDOW), (0, RADIUS_MAX))
-    flats = [block_form(rel_bias, *span, NEG) for span in spans]
-    masks = [block_form(used, *span, NEG)[0] for span in spans]
+    flat = block_form(rel_bias, NEG)
+    mask = block_form(used, NEG)[0]
     d = dilation_per_tile[0, 0]
     index = jnp.arange(depth, dtype=jnp.int32)
     turn = index // d
     slots = (d * (turn // BLOCK_ROWS) + index % d) * BLOCK_ROWS + turn % BLOCK_ROWS
     out = window_attention(
         jnp.full((16,), d, jnp.int32), slots.astype(jnp.int32), total_rows,
-        query_map, key_map, value_map, flats, masks, out_weight,
+        query_map, key_map, value_map, flat, mask, out_weight,
     )
     return out.reshape(depth, cols, out.shape[2])
 

time: 124 us -> 120 us (0.968)
  local copies, waits for them, and re-layouts: 9.55 us -> 6.1 us
    pad x3 -> x1, local copies, waits for them, and re-layouts: 2.29 us -> 0.82 us  [block_form(): jnp.pad(flat, ((0, 0), (0, -count % 8), (0, 0)), constant_values=fill)]
where the time goes in v3:
time: 120 us
  Pallas kernels  111 us (92%)
  local copies, waits for them, and re-layouts  6.1 us (5%)
  other arithmetic  1.65 us (1%)
  between operations  1.33 us (1%)
    pallas_call x1, Pallas kernels, window_attention(): pl.pallas_call(functools.partial(window_kernel, total_rows, groups), in_s...  111 us
    unnamed x2, local copies, waits for them, and re-layouts  3.75 us

profile of v3, /device:TPU:40, one launch (start us, length us, event | category | flops | bytes accessed | tf_op | source)
XLA Modules:
  0.0 119.8 jit_solution(13240888091305919547)
XLA Ops:
  1.3 0.6 fusion.5.slots
  1.9 0.6 broadcast_in_dim.16.d_own
  2.5 0.8 select_bitcast_fusion
  3.3 0.1 select_maximum_fusion.2
  3.4 0.1 copy.14
  3.5 0.6 pad_bitcast_fusion.m_o
  4.1 1.1 copy.11
  5.1 0.2 select_maximum_fusion
  5.3 0.2 copy.12
  5.6 0.8 pad.35.flat
  6.4 110.7 %window_attention.1 = bf16[4,128,1536]{2,1,0:T(8,128)(2,1)} custom-call(s32[16]{0:T(128)} %broadcast_in_dim.16.d_own, s32[16]{0:T(128)} %fusion.5.slots, bf16[16,32,1536]{2,1,0:T(8,128)(2,1)} %q_ref.1, bf16[16,32,1536]{2,1,0:T(8,128)(2,1)} %k_own.1, bf16[16,32,1536]{2,1,0:T(8,128)(2,1)} %v_own.1, f32[24,40,16]{2,1,0:T(8,128)} %pad.35.flat, ...), custom_call_target="tpu_custom_call" | custom-call | flops 20000000000 | bytes 40000000 | tf_op jit(solution)/shard_map/window_attention/pallas_call | solution.py:452
  117.1 2.7 %copy.27 = bf16[16,32,1536]{2,1,0:T(8,128)(2,1)} copy(bf16[16,32,1536]{2,1,0:T(8,128)(2,1)} %bitcast.22) | data formatting | bytes 3145728
  (1 shorter events, 0.0 us)
